TPU v7x, 32 devices: a whole 2x2x4 slice. The times are simulated.
32 devices in a mesh: dp: 4 (over y, x), frame: 2 (over core), tensor: 4 (over z).
Axes of the slice: x: 2, y: 2, z: 4, core: 2. Of those that a mesh axis runs over, the one named last changes fastest.
Arguments:
- tokens: bfloat16 [8, 8, 256, 1024], P('dp', ('frame', 'tensor')), may hold values from -6 to 6
- out_grad: bfloat16 [8, 8, 256, 1024], P('dp', ('frame', 'tensor')), may hold values from -6 to 6
- noise_index: int32 [8, 8], P('dp', 'frame'), may hold values from 0 to 999, as said below
- qkv_weight: bfloat16 [1024, 3, 1024], P(('dp', 'frame'), None, 'tensor'), may hold values from -0.1875 to 0.1875
- out_weight: bfloat16 [1024, 1024], P(('dp', 'frame'), 'tensor'), may hold values from -0.75 to 0.75
- up_weight: bfloat16 [1024, 4096], P(('dp', 'frame'), 'tensor'), may hold values from -0.1875 to 0.1875
- down_weight: bfloat16 [1024, 4096], P(('dp', 'frame'), 'tensor'), may hold values from -0.09375 to 0.09375
- ada_weight: bfloat16 [1024, 6, 1024], P(('dp', 'frame'), None, 'tensor'), may hold values from -0.25 to 0.25
Outputs:
- result: bfloat16 [8, 8, 256, 1024], P('dp', ('frame', 'tensor'))
- input_grad: bfloat16 [8, 8, 256, 1024], P('dp', ('frame', 'tensor'))
- qkv_grad: float32 [1024, 3, 1024], P(('dp', 'frame'), None, 'tensor')
- out_weight_grad: float32 [1024, 1024], P(('dp', 'frame'), 'tensor')
- up_grad: float32 [1024, 4096], P(('dp', 'frame'), 'tensor')
- down_grad: float32 [1024, 4096], P(('dp', 'frame'), 'tensor')
- ada_grad: float32 [1024, 6, 1024], P(('dp', 'frame'), None, 'tensor')
Inputs may be any that keep to these rules, and one draw needn't show every extreme that they name: `noise_index`: each frame's noise level, most often near 1000 - 1.
All inputs are finite; a program needn't handle non-finite values.
Results may differ from a plain program's by a relative error of at most 0.018.
Values may be sent and summed in bfloat16 or wider, within the bound.
A program may use at most 192 MiB of HBM per device.

v0:
```python
import math
import jax
import jax.numpy as jnp
from jax import lax
from jax.sharding import PartitionSpec as P

HEAD_DIM = 64
epsilon = 1e-06
highest = lax.Precision.HIGHEST


def normalize(values):
    center = values - jnp.mean(values, axis=-1, keepdims=True)
    spread = jnp.mean(center * center, axis=-1, keepdims=True)
    inverse = lax.rsqrt(spread + epsilon)
    return (center * inverse, inverse)


def norm_back(upstream, normed, inverse):
    upstream_mean = jnp.mean(upstream, axis=-1, keepdims=True)
    product_mean = jnp.mean(upstream * normed, axis=-1, keepdims=True)
    return inverse * (upstream - upstream_mean - normed * product_mean)


def level_embedding(levels, model_width):
    halfway = model_width // 2
    frequency = jnp.exp(-math.log(10000.0) * jnp.arange(halfway, dtype=jnp.float32) / halfway)
    angles = levels.astype(jnp.float32)[..., None] * frequency
    return jnp.concatenate([jnp.cos(angles), jnp.sin(angles)], axis=-1)


def gelu_tanh(values):
    return jax.nn.gelu(values, approximate=True)


def on_device(
    tokens, out_grad, noise_index, qkv_weight, out_weight, up_weight, down_weight, ada_weight
):
    clips = tokens.shape[0]
    patches = tokens.shape[2]
    model_width = tokens.shape[-1]
    local_width = qkv_weight.shape[2]
    rows_here = qkv_weight.shape[0]
    heads_here = local_width // HEAD_DIM
    scaling = HEAD_DIM ** (-0.5)
    groups = lax.axis_size("tensor")
    halves = lax.axis_size("frame")
    replicas = lax.axis_size("dp")
    with jax.named_scope("modulation"):
        levels_all = lax.all_gather(noise_index, ("dp", "frame"), axis=0, tiled=True)
        levels_all = levels_all.reshape(replicas * halves, clips, groups)
        condition_all = jax.nn.silu(level_embedding(levels_all, model_width)).astype(jnp.bfloat16)
        row_block = lax.axis_index("dp") * halves + lax.axis_index("frame")
        my_condition = lax.dynamic_slice_in_dim(
            condition_all, row_block * rows_here, rows_here, axis=3
        )
        partial_mod = jnp.einsum(
            "acgd,dkw->acgkw", my_condition, ada_weight, preferred_element_type=jnp.float32
        )
        summed_mod = jnp.sum(lax.all_to_all(partial_mod, ("dp", "frame"), 0, 0, tiled=True), axis=0)
        group_mod = lax.all_gather(summed_mod, "tensor", axis=3, tiled=True)
        group_mod = jnp.swapaxes(group_mod, 1, 2)[:, :, :, None, :]
        group_index = lax.axis_index("tensor")
        modulation = lax.dynamic_index_in_dim(group_mod, group_index, axis=2, keepdims=False)
    with jax.named_scope("weights"):
        joint_weight, mixer_weight, upward_weight, downward_weight = (
            lax.all_gather(w, ("dp", "frame"), axis=0, tiled=True)
            for w in (qkv_weight, out_weight, up_weight, down_weight)
        )
    residual = tokens[:, 0].astype(jnp.float32)
    upstream = out_grad[:, 0].astype(jnp.float32)
    with jax.named_scope("group_inputs"):
        group_tokens = lax.all_gather(tokens[:, 0], "tensor", axis=1, tiled=True)
        group_upstream = lax.all_gather(out_grad[:, 0], "tensor", axis=1, tiled=True)

    def gather_halves(values):
        if halves != 2:
            return lax.all_gather(values, "frame", axis=1, tiled=True)
        other = lax.ppermute(values, "frame", [(0, 1), (1, 0)])
        return jnp.concatenate([values, other], axis=1)

    def scatter_halves(values):
        if halves != 2:
            return lax.psum_scatter(
                values.astype(jnp.bfloat16), "frame", scatter_dimension=1, tiled=True
            ).astype(jnp.float32)
        count = values.shape[1] // 2
        mine = values[:, :count]
        other = lax.ppermute(values[:, count:].astype(jnp.bfloat16), "frame", [(0, 1), (1, 0)])
        return mine.astype(jnp.bfloat16).astype(jnp.float32) + other.astype(jnp.float32)

    def clip_pass(residual, upstream, modulation, group_tokens, group_upstream, group_mod):
        clips = residual.shape[0]
        patches = residual.shape[1]
        shift1, scale1, gate1 = (modulation[:, 0], modulation[:, 1], modulation[:, 2])
        shift2, scale2, gate2 = (modulation[:, 3], modulation[:, 4], modulation[:, 5])

        def gather_tokens(values):
            return lax.all_gather(values, "tensor", axis=1, tiled=True)

        def scatter_tokens(values):
            parts = values.astype(jnp.bfloat16).reshape(
                values.shape[0], groups, -1, values.shape[-1]
            )
            received = lax.all_to_all(parts, "tensor", 1, 1, tiled=True)
            return jnp.sum(received.astype(jnp.float32), axis=1)

        with jax.named_scope("forward"):
            normed_one, inverse_one = normalize(residual)
            group_normed, _ = normalize(
                group_tokens.astype(jnp.float32).reshape(clips, groups, patches, model_width)
            )
            flat_one = (
                (group_normed * (1.0 + group_mod[:, 1]) + group_mod[:, 0])
                .astype(jnp.bfloat16)
                .reshape(clips, groups * patches, model_width)
            )
            token_count = flat_one.shape[1]
            projected = jnp.einsum(
                "crd,dkh->crkh", flat_one, joint_weight, preferred_element_type=jnp.float32
            ).astype(jnp.bfloat16)
            queries = projected[:, :, 0]
            keys_all = gather_halves(projected[:, :, 1])
            values_all = gather_halves(projected[:, :, 2])
            key_heads = keys_all.reshape(clips, -1, heads_here, HEAD_DIM)
            value_heads = values_all.reshape(clips, -1, heads_here, HEAD_DIM)
            block_rows = min(512, token_count)
            block_count = token_count // block_rows
            query_blocks = jnp.moveaxis(
                queries.reshape(clips, block_count, block_rows, heads_here, HEAD_DIM), 1, 0
            )

            def attend(query_block):
                scores = (
                    jnp.einsum(
                        "cqhe,ckhe->chqk",
                        query_block,
                        key_heads,
                        preferred_element_type=jnp.float32,
                    )
                    * scaling
                )
                largest = jnp.max(scores, axis=-1, keepdims=True)
                raised = jnp.exp(scores - largest)
                totals_row = jnp.sum(raised, axis=-1, keepdims=True)
                probs_low = (raised / totals_row).astype(jnp.bfloat16)
                outputs = jnp.einsum(
                    "chqk,ckhe->cqhe", probs_low, value_heads, preferred_element_type=jnp.float32
                )
                return (outputs.astype(jnp.bfloat16), (largest + jnp.log(totals_row))[..., 0])

            attended_blocks, log_totals = lax.map(attend, query_blocks)
            attended = jnp.moveaxis(attended_blocks, 0, 1).reshape(clips, token_count, local_width)
            partial_one = jnp.einsum(
                "crh,oh->cro", attended, mixer_weight, preferred_element_type=jnp.float32
            )
            branch_one = scatter_tokens(partial_one)
            middle = residual + gate1 * branch_one
            normed_two, inverse_two = normalize(middle)
            entering_two = (normed_two * (1.0 + scale2) + shift2).astype(jnp.bfloat16)
            flat_two = gather_tokens(entering_two)
            up_values = jnp.einsum(
                "crd,df->crf", flat_two, upward_weight, preferred_element_type=jnp.float32
            )
            hidden = gelu_tanh(up_values).astype(jnp.bfloat16)
            partial_two = jnp.einsum(
                "crf,of->cro", hidden, downward_weight, preferred_element_type=jnp.float32
            )
            branch_two = scatter_tokens(partial_two)
            output = (middle + gate2 * branch_two).astype(jnp.bfloat16)
        with jax.named_scope("backward_ffn"):
            grad_gate_two = jnp.sum(upstream * branch_two, axis=1)
            grad_two_all = (
                (
                    group_mod[:, 5]
                    * group_upstream.astype(jnp.float32).reshape(
                        clips, groups, patches, model_width
                    )
                )
                .astype(jnp.bfloat16)
                .reshape(clips, groups * patches, model_width)
            )
            grad_hidden = jnp.einsum(
                "cro,of->crf", grad_two_all, downward_weight, preferred_element_type=jnp.float32
            )
            down_total = jnp.einsum(
                "cro,crf->of", grad_two_all, hidden, preferred_element_type=jnp.float32
            )
            _, gelu_pullback = jax.vjp(gelu_tanh, up_values)
            grad_up = gelu_pullback(grad_hidden)[0].astype(jnp.bfloat16)
            up_total = jnp.einsum(
                "crd,crf->df", flat_two, grad_up, preferred_element_type=jnp.float32
            )
            partial_back_two = jnp.einsum(
                "crf,df->crd", grad_up, upward_weight, preferred_element_type=jnp.float32
            )
            grad_entering_two = scatter_tokens(partial_back_two)
            grad_shift_two = jnp.sum(grad_entering_two, axis=1)
            grad_scale_two = jnp.sum(grad_entering_two * normed_two, axis=1)
            grad_middle = upstream + norm_back(
                grad_entering_two * (1.0 + scale2), normed_two, inverse_two
            )
            grad_gate_one = jnp.sum(grad_middle * branch_one, axis=1)
        with jax.named_scope("backward_attention"):
            grad_branch_one = (gate1 * grad_middle).astype(jnp.bfloat16)
            grad_one_all = gather_tokens(grad_branch_one)
            grad_attended = jnp.einsum(
                "cro,oh->crh", grad_one_all, mixer_weight, preferred_element_type=jnp.float32
            ).astype(jnp.bfloat16)
            mixer_total = jnp.einsum(
                "cro,crh->oh", grad_one_all, attended, preferred_element_type=jnp.float32
            )
            grad_blocks = jnp.moveaxis(
                grad_attended.reshape(clips, block_count, block_rows, heads_here, HEAD_DIM), 1, 0
            )

            def attend_back(carried, pieces):
                key_sum, value_sum = carried
                query_block, grad_block, log_block = pieces
                scores = (
                    jnp.einsum(
                        "cqhe,ckhe->chqk",
                        query_block,
                        key_heads,
                        preferred_element_type=jnp.float32,
                    )
                    * scaling
                )
                probs = jnp.exp(scores - log_block[..., None])
                grad_probs = jnp.einsum(
                    "cqhe,ckhe->chqk", grad_block, value_heads, preferred_element_type=jnp.float32
                )
                value_sum = value_sum + jnp.einsum(
                    "chqk,cqhe->ckhe",
                    probs.astype(jnp.bfloat16),
                    grad_block,
                    preferred_element_type=jnp.float32,
                )
                row_terms = jnp.sum(probs * grad_probs, axis=-1, keepdims=True)
                grad_scores = (probs * (grad_probs - row_terms)).astype(jnp.bfloat16)
                grad_queries = (
                    jnp.einsum(
                        "chqk,ckhe->cqhe",
                        grad_scores,
                        key_heads,
                        preferred_element_type=jnp.float32,
                    )
                    * scaling
                )
                key_sum = (
                    key_sum
                    + jnp.einsum(
                        "chqk,cqhe->ckhe",
                        grad_scores,
                        query_block,
                        preferred_element_type=jnp.float32,
                    )
                    * scaling
                )
                return ((key_sum, value_sum), grad_queries)

            zeros_keys = jnp.zeros(key_heads.shape, jnp.float32)
            (key_grads, value_grads), query_grads = lax.scan(
                attend_back, (zeros_keys, zeros_keys), (query_blocks, grad_blocks, log_totals)
            )
            query_grads = jnp.moveaxis(query_grads, 0, 1).reshape(clips, token_count, local_width)
            key_own, value_own = (
                scatter_halves(grads.reshape(clips, -1, local_width))
                for grads in (key_grads, value_grads)
            )
            grad_projected = jnp.stack([query_grads, key_own, value_own], axis=2).astype(
                jnp.bfloat16
            )
            joint_total = jnp.einsum(
                "crd,crkh->dkh", flat_one, grad_projected, preferred_element_type=jnp.float32
            )
            partial_back_one = jnp.einsum(
                "crkh,dkh->crd", grad_projected, joint_weight, preferred_element_type=jnp.float32
            )
            grad_entering_one = scatter_tokens(partial_back_one)
            grad_shift_one = jnp.sum(grad_entering_one, axis=1)
            grad_scale_one = jnp.sum(grad_entering_one * normed_one, axis=1)
            grad_input = grad_middle + norm_back(
                grad_entering_one * (1.0 + scale1), normed_one, inverse_one
            )
        grad_modulation = jnp.stack(
            [
                grad_shift_one,
                grad_scale_one,
                grad_gate_one,
                grad_shift_two,
                grad_scale_two,
                grad_gate_two,
            ],
            axis=1,
        )
        totals = (joint_total, mixer_total, up_total, down_total)
        return (output, grad_input.astype(jnp.bfloat16), grad_modulation, totals)

    pieces = [
        clip_pass(
            residual[i : i + 1],
            upstream[i : i + 1],
            modulation[i : i + 1],
            group_tokens[i : i + 1],
            group_upstream[i : i + 1],
            group_mod[i : i + 1],
        )
        for i in range(clips)
    ]
    output = jnp.concatenate([p[0] for p in pieces], axis=0)
    grad_input_low = jnp.concatenate([p[1] for p in pieces], axis=0)
    grad_modulation = jnp.concatenate([p[2] for p in pieces], axis=0)
    joint_total, mixer_total, up_total, down_total = (
        sum((p[3][k] for p in pieces[1:])) + pieces[0][3][k] for k in range(4)
    )
    with jax.named_scope("ada_grad"):
        grad_columns = lax.all_to_all(
            grad_modulation.reshape(clips, 1, 6, model_width), "tensor", 3, 1, tiled=True
        )
        grad_all = lax.all_gather(grad_columns, ("dp", "frame"), axis=0, tiled=True)
        grad_all = grad_all.reshape(replicas * halves, clips, groups, 6, local_width)
        adaptive_total = jnp.einsum(
            "acgd,acgkw->dkw", my_condition.astype(jnp.float32), grad_all, precision=highest
        )
    with jax.named_scope("weight_grads"):
        summed = tuple(
            (
                lax.psum_scatter(
                    total.astype(jnp.bfloat16), ("dp", "frame"), scatter_dimension=0, tiled=True
                ).astype(jnp.float32)
                for total in (joint_total, mixer_total, up_total, down_total)
            )
        )
    result = output[:, None]
    input_grad = grad_input_low[:, None]
    return (result, input_grad, summed[0], summed[1], summed[2], summed[3], adaptive_total)


def solution(mesh):
    return jax.shard_map(
        on_device,
        mesh=mesh,
        in_specs=(
            P("dp", ("frame", "tensor"), None, None),
            P("dp", ("frame", "tensor"), None, None),
            P("dp", "frame"),
            P(("dp", "frame"), None, "tensor"),
            P(("dp", "frame"), "tensor"),
            P(("dp", "frame"), "tensor"),
            P(("dp", "frame"), "tensor"),
            P(("dp", "frame"), None, "tensor"),
        ),
        out_specs=(
            P("dp", ("frame", "tensor"), None, None),
            P("dp", ("frame", "tensor"), None, None),
            P(("dp", "frame"), None, "tensor"),
            P(("dp", "frame"), "tensor"),
            P(("dp", "frame"), "tensor"),
            P(("dp", "frame"), "tensor"),
            P(("dp", "frame"), None, "tensor"),
        ),
        check_vma=False,
    )
```

profile of v0, /device:TPU:0, one launch (start us, length us, event | category | flops | bytes accessed | tf_op | source)
XLA Modules:
  0.0 1021.4 jit_solution(15384394116283009315)
XLA Ops:
  10.5 10.6 %all-gather.3 = s32[8,2,4]{2,1,0:T(2,128)S(1)} all-gather(s32[1,2,4]{2,1,0:T(2,128)} %bitcast.739), channel_id=1, replica_groups=mesh['dp'=4,'frame'=2,'tensor'=4] {'dp','frame'}, dimensions={0}, use_global_device_ids=true | all-gather | bytes 288 | tf_op jit(solution)/shard_map/modulation/all_gather | solution.py:50
  27.3 12.8 %all_gather.43 = bf16[1024,256]{1,0:T(8,128)(2,1)} all-gather(bf16[128,256]{1,0:T(8,128)(2,1)S(1)} %copy-done.71), channel_id=1, replica_groups=mesh['dp'=4,'frame'=2,'tensor'=4] {'dp','frame'}, dimensions={0}, use_global_device_ids=true | all-gather | bytes 589824 | tf_op jit(solution)/shard_map/weights/all_gather | solution.py:67
  40.3 19.4 %all_gather.40 = f32[2,4,6,1024]{3,2,1,0:T(8,128)S(1)} all-gather(f32[2,4,6,256]{3,2,1,0:T(8,128)S(1)} %copy.337), channel_id=1, replica_groups=mesh['dp'=4,'frame'=2,'tensor'=4] {'tensor'}, dimensions={3}, use_global_device_ids=true | all-gather | bytes 245760 | tf_op jit(solution)/shard_map/modulation/all_gather | solution.py:61
  61.0 36.2 %all-gather.28.cloned.1.call-done = bf16[2,1,1024,1024]{3,2,1,0:T(8,128)(2,1)} async-done(((bf16[2,1,256,1024]{3,2,1,0:T(8,128)(2,1)}), bf16[2,1,1024,1024]{3,2,1,0:T(8,128)(2,1)}) %all-gather.28.cloned.1.call-update) | async-done | bytes 4194320 | tf_op jit(solution)/shard_map/group_inputs/all_gather | solution.py:73
  107.8 16.2 %all-gather.14.cloned.1.call-done = bf16[1024,3,256]{0,2,1:T(8,128)(2,1)} async-done(((bf16[128,3,256]{0,2,1:T(8,128)(2,1)}), bf16[1024,3,256]{0,2,1:T(8,128)(2,1)}) %all-gather.14.cloned.1.call-update) | async-done | bytes 1572880 | tf_op jit(solution)/shard_map/weights/all_gather | solution.py:67
  140.7 21.9 %while.55 = (s32[]{:T(128)}, bf16[2,1,512,4,64]{2,4,3,1,0:T(8,128)(2,1)}, f32[2,1,4,512]{3,2,1,0:T(4,128)S(1)}, bf16[2,1,512,4,64]{2,4,3,1,0:T(8,128)(2,1)S(1)},...) while((s32[]{:T(128)}, ...), condition=%wide.region_16.17_spmd, body=%wide.region_13.16_spmd.sunk | while | flops 1111619584 | bytes 53019220 | solution.py:152
  157.3 5.1 fusion.283
  174.9 21.8 %while.54 = (s32[]{:T(128)}, bf16[2,1,512,4,64]{2,4,3,1,0:T(8,128)(2,1)}, f32[2,1,4,512]{3,2,1,0:T(4,128)S(1)}, bf16[2,1,512,4,64]{2,4,3,1,0:T(8,128)(2,1)S(1)},...) while((s32[]{:T(128)}, bf16[2,1,512,4,64]{2,4,3,1,0:T(8,128)(2,1)}, ...), condition=%wide.region_6.7_spmd, body=%wide.region_3.0_spmd.sunk | while | flops 1111619584 | bytes 53019220 | solution.py:152
  201.6 49.2 %all-to-all-done.3 = bf16[1,4,256,1024]{3,2,0,1:T(8,128)(2,1)} async-done(((bf16[1,4,256,1024]{3,2,0,1:T(8,128)(2,1)}), bf16[1,4,256,1024]{3,2,0,1:T(8,128)(2,1)}, u32[]{:S(2)}, u32[]{:S(2)}) %all-to-all-start.3) | async-done | bytes 2097184 | tf_op jit(solution)/shard_map/forward/all_to_all | solution.py:105
  261.7 42.4 %all-to-all-done.1 = bf16[1,4,256,1024]{3,2,0,1:T(8,128)(2,1)} async-done(((bf16[1,4,256,1024]{3,2,0,1:T(8,128)(2,1)}), bf16[1,4,256,1024]{3,2,0,1:T(8,128)(2,1)}, u32[]{:S(2)}, u32[]{:S(2)}) %all-to-all-start.1) | async-done | bytes 2097184 | tf_op jit(solution)/shard_map/forward/all_to_all | solution.py:105
  312.2 5.6 fusion.107
  317.8 6.9 fusion.211
  326.0 30.3 %all-gather.22.cloned.1.call-done = bf16[1,1024,1024]{2,1,0:T(8,128)(2,1)} async-done(((bf16[1,256,1024]{2,1,0:T(8,128)(2,1)}), bf16[1,1024,1024]{2,1,0:T(8,128)(2,1)}) %all-gather.22.cloned.1.call-update) | async-done | bytes 2097168 | tf_op jit(solution)/shard_map/forward/all_gather | solution.py:99
  356.3 10.1 fusion.125
  374.9 6.6 fusion.210
  381.6 56.0 %all-gather.16.cloned.1.call-done = bf16[1,1024,1024]{2,1,0:T(8,128)(2,1)} async-done(((bf16[1,256,1024]{2,1,0:T(8,128)(2,1)}), bf16[1,1024,1024]{2,1,0:T(8,128)(2,1)}) %all-gather.16.cloned.1.call-update) | async-done | bytes 2097168 | tf_op jit(solution)/shard_map/forward/all_gather | solution.py:99
  437.6 10.1 fusion.118
  457.2 6.9 convolution_convert_fusion.2
  464.2 39.3 %all-to-all-done.5 = bf16[1,4,256,1024]{3,2,0,1:T(8,128)(2,1)} async-done(((bf16[1,4,256,1024]{3,2,0,1:T(8,128)(2,1)}), bf16[1,4,256,1024]{3,2,0,1:T(8,128)(2,1)}, u32[]{:S(2)}, u32[]{:S(2)}) %all-to-all-start.5) | async-done | bytes 2097184 | tf_op jit(solution)/shard_map/backward_ffn/all_to_all | solution.py:105
  509.6 6.9 convolution_convert_fusion.4
  516.5 39.3 %all-to-all-done.4 = bf16[1,4,256,1024]{3,2,0,1:T(8,128)(2,1)} async-done(((bf16[1,4,256,1024]{3,2,0,1:T(8,128)(2,1)}), bf16[1,4,256,1024]{3,2,0,1:T(8,128)(2,1)}, u32[]{:S(2)}, u32[]{:S(2)}) %all-to-all-start.4) | async-done | bytes 2097184 | tf_op jit(solution)/shard_map/forward/all_to_all | solution.py:105
  574.4 67.3 %all-to-all-done.2 = bf16[1,4,256,1024]{3,2,0,1:T(8,128)(2,1)} async-done(((bf16[1,4,256,1024]{3,2,0,1:T(8,128)(2,1)}), bf16[1,4,256,1024]{3,2,0,1:T(8,128)(2,1)}, u32[]{:S(2)}, u32[]{:S(2)}) %all-to-all-start.2) | async-done | bytes 2097184 | tf_op jit(solution)/shard_map/forward/all_to_all | solution.py:105
  653.4 5.2 fusion.197
  680.0 87.2 %while.57 = (s32[]{:T(128)}, f32[1,2048,4,64]{1,3,2,0:T(8,128)}, f32[1,2048,4,64]{1,3,2,0:T(8,128)}, bf16[2,1,512,4,64]{2,4,3,1,0:T(8,128)(2,1)}, bf16[2,1,512,4...) while((s32[]{:T(128)}, f32[1,2048,4,64]{1,3,2,0:T(8,128)}, ...), condition=%wide.region_39.40_spmd.clone, body=%wide.region_37.39_spmd.clone.sunk | while | flops 2737436672 | bytes 273212096 | solution.py:263
  682.5 8.6 multiply_reduce_fusion.23
  693.3 10.6 %multiply_convert_fusion.14 = bf16[4,512,2048]{2,1,0:T(8,128)(2,1)} fusion(f32[4,512,2048]{2,1,0:T(8,128)} %get-tuple-element.848, f32[4,512,2048]{2,1,0:T(8,128)S(1)} %fusion.304, f32[4,512]{1,0:T(4,128)S(1)} %get-tuple-element.849, f32[4,512]{1,0:T(4,128)S(1)} %dynamic-slice_bitcast_fusion.7), kind=kLoop, calls=%fused_computation.66.clone.1 | loop fusion | flops 20971520 | bytes 41959424 | tf_op jit(solution)/shard_map/backward_attention/while/body/eval_jaxpr/convert_element_type | solution.py:240
  703.9 6.9 fusion.305
  710.8 7.5 fusion.307
  725.1 8.6 multiply_reduce_fusion.23
  736.0 10.4 %multiply_convert_fusion.14 = bf16[4,512,2048]{2,1,0:T(8,128)(2,1)} fusion(f32[4,512,2048]{2,1,0:T(8,128)} %get-tuple-element.848, f32[4,512,2048]{2,1,0:T(8,128)S(1)} %fusion.304, f32[4,512]{1,0:T(4,128)S(1)} %get-tuple-element.849, f32[4,512]{1,0:T(4,128)S(1)} %dynamic-slice_bitcast_fusion.7), kind=kLoop, calls=%fused_computation.66.clone.1 | loop fusion | flops 20971520 | bytes 41959424 | tf_op jit(solution)/shard_map/backward_attention/while/body/eval_jaxpr/convert_element_type | solution.py:240
  746.4 7.6 fusion.305
  754.0 7.5 fusion.307
  761.5 5.6 fusion.306
  793.5 86.0 %while.56 = (s32[]{:T(128)}, f32[1,2048,4,64]{1,3,2,0:T(8,128)}, f32[1,2048,4,64]{1,3,2,0:T(8,128)}, bf16[2,1,512,4,64]{2,4,3,1,0:T(8,128)(2,1)}, bf16[2,1,512,4...) while((s32[]{:T(128)}, f32[1,2048,4,64]{1,3,2,0:T(8,128)}, ...), condition=%wide.region_28.29_spmd.clone, body=%wide.region_26.28_spmd.clone.sunk | while | flops 2737436672 | bytes 273212096 | solution.py:263
  795.9 8.6 multiply_reduce_fusion.22
  806.8 10.4 %multiply_convert_fusion.13 = bf16[4,512,2048]{2,1,0:T(8,128)(2,1)} fusion(f32[4,512,2048]{2,1,0:T(8,128)} %get-tuple-element.837, f32[4,512,2048]{2,1,0:T(8,128)S(1)} %fusion.292, f32[4,512]{1,0:T(4,128)S(1)} %get-tuple-element.838, f32[4,512]{1,0:T(4,128)S(1)} %dynamic-slice_bitcast_fusion.6), kind=kLoop, calls=%fused_computation.32.clone.1 | loop fusion | flops 20971520 | bytes 41959424 | tf_op jit(solution)/shard_map/backward_attention/while/body/eval_jaxpr/convert_element_type | solution.py:240
  817.2 6.5 fusion.293
  823.7 7.5 fusion.295
  838.0 8.6 multiply_reduce_fusion.22
  848.9 10.4 %multiply_convert_fusion.13 = bf16[4,512,2048]{2,1,0:T(8,128)(2,1)} fusion(f32[4,512,2048]{2,1,0:T(8,128)} %get-tuple-element.837, f32[4,512,2048]{2,1,0:T(8,128)S(1)} %fusion.292, f32[4,512]{1,0:T(4,128)S(1)} %get-tuple-element.838, f32[4,512]{1,0:T(4,128)S(1)} %dynamic-slice_bitcast_fusion.6), kind=kLoop, calls=%fused_computation.32.clone.1 | loop fusion | flops 20971520 | bytes 41959424 | tf_op jit(solution)/shard_map/backward_attention/while/body/eval_jaxpr/convert_element_type | solution.py:240
  859.3 7.0 fusion.293
  866.3 7.5 fusion.295
  873.8 5.6 fusion.294
  908.1 5.1 all-to-all-start.6
  913.3 5.4 add_convert_fusion.2
  923.5 9.4 reduce-scatter.7.cloned.1.call-done
  934.5 40.2 %reduce-scatter.5.cloned.1.call-done = bf16[128,3,256]{2,0,1:T(8,128)(2,1)} async-done(((bf16[1024,3,256]{2,0,1:T(8,128)(2,1)}), bf16[128,3,256]{2,0,1:T(8,128)(2,1)}) %reduce-scatter.5.cloned.1.call-update) | async-done | bytes 196624 | tf_op jit(solution)/shard_map/weight_grads/reduce_scatter | solution.py:329
  1003.5 9.5 all-gather.2
  (452 shorter events, 307.8 us)
Async XLA Ops:
  7.2 20.2 %copy-start.71 = (bf16[128,256]{1,0:T(8,128)(2,1)S(1)}, bf16[128,256]{1,0:T(8,128)(2,1)}, u32[]{:S(2)}) copy-start(bf16[128,256]{1,0:T(8,128)(2,1)} %param.20) | copy-start | bytes 196612
  7.2 90.0 %all-gather.28.cloned.1.call-start = ((), (), s32[]{:S(2)}) async-start(), calls=%async_computation.25 | async-start | bytes 5242880 | tf_op jit(solution)/shard_map/group_inputs/all_gather | solution.py:73
  7.9 116.1 %all-gather.14.cloned.1.call-start = ((), (), s32[]{:S(2)}) async-start(), calls=%async_computation.14 | async-start | bytes 1769472 | tf_op jit(solution)/shard_map/weights/all_gather | solution.py:67
  9.7 302.4 %all-gather.30.cloned.1.call-start = ((), (), s32[]{:S(2)}) async-start(), calls=%async_computation.26 | async-start | bytes 5242880 | tf_op jit(solution)/shard_map/group_inputs/all_gather | solution.py:74
  23.3 16.9 %all-to-all-start = ((f32[8,2,4,6,256]{4,2,3,1,0:T(4,128)}), f32[8,2,4,6,256]{4,2,3,1,0:T(4,128)S(1)}, u32[]{:S(2)}, u32[]{:S(2)}) async-start(f32[8,2,4,6,256]{4,2,3,1,0:T(4,128)} %fusion.183), calls=%async_computation | async-start | bytes 786432 | tf_op jit(solution)/shard_map/modulation/all_to_all | solution.py:60
  26.8 291.0 %all-gather.20.cloned.1.call-start = ((), (), s32[]{:S(2)}) async-start(), calls=%async_computation.17 | async-start | bytes 2359296 | tf_op jit(solution)/shard_map/weights/all_gather | solution.py:67
  59.7 43.3 %copy-start.52 = (f32[2,4,6,1024]{3,2,1,0:T(8,128)}, f32[2,4,6,1024]{3,2,1,0:T(8,128)S(1)}, u32[]{:S(2)}) copy-start(f32[2,4,6,1024]{3,2,1,0:T(8,128)S(1)} %all_gather.40) | copy-start | bytes 589828
  128.5 8.0 collective-permute-start.3
  128.8 9.9 collective-permute-start.2
  134.8 36.8 %collective-permute-start.1 = (bf16[1,1024,256]{1,2,0:T(8,128)(2,1)}, bf16[1,1024,256]{1,2,0:T(8,128)(2,1)}, u32[]{:S(2)}, u32[]{:S(2)}) collective-permute-start(bf16[1,1024,256]{1,2,0:T(8,128)(2,1)} %get-tuple-element.602), channel_id=1, source_target_pairs={{0,4},{4,0},{1,5},{5,1},{2,6},{6,2},{3,7},{7,3},{8,12},{12,8},{9,1... | collective-permute-start | bytes 1572872 | tf_op jit(solution)/shard_map/forward/ppermute | solution.py:79
  135.1 37.9 %collective-permute-start = (bf16[1,1024,256]{1,2,0:T(8,128)(2,1)}, bf16[1,1024,256]{1,2,0:T(8,128)(2,1)}, u32[]{:S(2)}, u32[]{:S(2)}) collective-permute-start(bf16[1,1024,256]{1,2,0:T(8,128)(2,1)} %get-tuple-element.601), channel_id=1, source_target_pairs={{0,4},{4,0},{1,5},{5,1},{2,6},{6,2},{3,7},{7,3},{8,12},{12,8},{9,1... | collective-permute-start | bytes 1572872 | tf_op jit(solution)/shard_map/forward/ppermute | solution.py:79
  140.7 24.1 %copy-start.36 = (bf16[1024,256]{1,0:T(8,128)(2,1)S(1)}, bf16[1024,256]{1,0:T(8,128)(2,1)}, u32[]{:S(2)}) copy-start(bf16[1024,256]{1,0:T(8,128)(2,1)} %all_gather.43) | copy-start | bytes 1572868
  166.9 83.9 %all-to-all-start.3 = ((bf16[1,4,256,1024]{3,2,0,1:T(8,128)(2,1)}), bf16[1,4,256,1024]{3,2,0,1:T(8,128)(2,1)}, u32[]{:S(2)}, u32[]{:S(2)}) async-start(bf16[1,4,256,1024]{3,2,0,1:T(8,128)(2,1)} %bitcast.675), calls=%async_computation.3 | async-start | bytes 4194304 | tf_op jit(solution)/shard_map/forward/all_to_all | solution.py:105
  174.9 24.6 %copy-start.37 = (bf16[1024,256]{1,0:T(8,128)(2,1)S(1)}, bf16[1024,256]{1,0:T(8,128)(2,1)}, u32[]{:S(2)}) copy-start(bf16[1024,256]{1,0:T(8,128)(2,1)} %all_gather.43) | copy-start | bytes 1572868
  196.7 54.1 %copy-start.63 = (f32[2,1,4,512]{3,2,1,0:T(4,128)}, f32[2,1,4,512]{3,2,1,0:T(4,128)S(1)}, u32[]{:S(2)}) copy-start(f32[2,1,4,512]{3,2,1,0:T(4,128)S(1)} %get-tuple-element.898) | copy-start | bytes 49156
  196.7 54.1 %copy-start.6 = (bf16[1,2048,4,64]{1,3,2,0:T(8,128)(2,1)}, bf16[1,2048,4,64]{1,3,2,0:T(8,128)(2,1)S(1)}, u32[]{:S(2)}) copy-start(bf16[1,2048,4,64]{1,3,2,0:T(8,128)(2,1)S(1)} %get-tuple-element.971) | copy-start | bytes 3145732
  196.7 54.1 %copy-start.10 = (bf16[1,2048,4,64]{1,3,2,0:T(8,128)(2,1)}, bf16[1,2048,4,64]{1,3,2,0:T(8,128)(2,1)S(1)}, u32[]{:S(2)}) copy-start(bf16[1,2048,4,64]{1,3,2,0:T(8,128)(2,1)S(1)} %get-tuple-element.973) | copy-start | bytes 3145732
  250.8 53.2 %all-to-all-start.1 = ((bf16[1,4,256,1024]{3,2,0,1:T(8,128)(2,1)}), bf16[1,4,256,1024]{3,2,0,1:T(8,128)(2,1)}, u32[]{:S(2)}, u32[]{:S(2)}) async-start(bf16[1,4,256,1024]{3,2,0,1:T(8,128)(2,1)} %bitcast.676), calls=%async_computation.1 | async-start | bytes 4194304 | tf_op jit(solution)/shard_map/forward/all_to_all | solution.py:105
  255.4 70.6 %all-gather.18.cloned.1.call-start = ((), (), s32[]{:S(2)}) async-start(), calls=%async_computation.16 | async-start | bytes 2359296 | tf_op jit(solution)/shard_map/weights/all_gather | solution.py:67
  256.0 100.3 %all-gather.22.cloned.1.call-start = ((), (), s32[]{:S(2)}) async-start(), calls=%async_computation.18 | async-start | bytes 2621440 | tf_op jit(solution)/shard_map/forward/all_gather | solution.py:99
  257.6 48.6 %copy-start.16 = (f32[2,1,256,1024]{3,2,1,0:T(8,128)}, f32[2,1,256,1024]{3,2,1,0:T(8,128)S(1)}, u32[]{:S(2)}) copy-start(f32[2,1,256,1024]{3,2,1,0:T(8,128)S(1)} %convert_element_type.357) | copy-start | bytes 6291460
  257.8 52.1 %copy-start.72 = (f32[256]{0:T(256)}, f32[256]{0:T(256)S(1)}, u32[]{:S(2)}) copy-start(f32[256]{0:T(256)S(1)} %get-tuple-element.646) | copy-start | bytes 3076
  257.8 52.1 %copy-start.74 = (f32[256]{0:T(256)}, f32[256]{0:T(256)S(1)}, u32[]{:S(2)}) copy-start(f32[256]{0:T(256)S(1)} %get-tuple-element.647) | copy-start | bytes 3076
  311.2 126.3 %all-gather.16.cloned.1.call-start = ((), (), s32[]{:S(2)}) async-start(), calls=%async_computation.15 | async-start | bytes 2621440 | tf_op jit(solution)/shard_map/forward/all_gather | solution.py:99
  370.1 82.7 %all-to-all-start.7 = ((bf16[1,4,256,1024]{3,2,0,1:T(8,128)(2,1)}), bf16[1,4,256,1024]{3,2,0,1:T(8,128)(2,1)}, u32[]{:S(2)}, u32[]{:S(2)}) async-start(bf16[1,4,256,1024]{3,2,0,1:T(8,128)(2,1)} %bitcast.687), calls=%async_computation.7 | async-start | bytes 4194304 | tf_op jit(solution)/shard_map/backward_ffn/all_to_all | solution.py:105
  452.7 50.7 %all-to-all-start.5 = ((bf16[1,4,256,1024]{3,2,0,1:T(8,128)(2,1)}), bf16[1,4,256,1024]{3,2,0,1:T(8,128)(2,1)}, u32[]{:S(2)}, u32[]{:S(2)}) async-start(bf16[1,4,256,1024]{3,2,0,1:T(8,128)(2,1)} %bitcast.689), calls=%async_computation.5 | async-start | bytes 4194304 | tf_op jit(solution)/shard_map/backward_ffn/all_to_all | solution.py:105
  464.2 43.9 %copy-start.40 = (bf16[2,1,256,1024]{3,2,1,0:T(8,128)(2,1)S(1)}, bf16[2,1,256,1024]{3,2,1,0:T(8,128)(2,1)}, u32[]{:S(2)}) copy-start(bf16[2,1,256,1024]{3,2,1,0:T(8,128)(2,1)} %param.17) | copy-start | bytes 3145732
  503.4 52.4 %all-to-all-start.4 = ((bf16[1,4,256,1024]{3,2,0,1:T(8,128)(2,1)}), bf16[1,4,256,1024]{3,2,0,1:T(8,128)(2,1)}, u32[]{:S(2)}, u32[]{:S(2)}) async-start(bf16[1,4,256,1024]{3,2,0,1:T(8,128)(2,1)} %bitcast.688), calls=%async_computation.4 | async-start | bytes 4194304 | tf_op jit(solution)/shard_map/forward/all_to_all | solution.py:105
  555.8 85.9 %all-to-all-start.2 = ((bf16[1,4,256,1024]{3,2,0,1:T(8,128)(2,1)}), bf16[1,4,256,1024]{3,2,0,1:T(8,128)(2,1)}, u32[]{:S(2)}, u32[]{:S(2)}) async-start(bf16[1,4,256,1024]{3,2,0,1:T(8,128)(2,1)} %bitcast.686), calls=%async_computation.2 | async-start | bytes 4194304 | tf_op jit(solution)/shard_map/forward/all_to_all | solution.py:105
  560.3 110.8 %all-gather.26.cloned.1.call-start = ((), (), s32[]{:S(2)}) async-start(), calls=%async_computation.20 | async-start | bytes 2621440 | tf_op jit(solution)/shard_map/backward_attention/all_gather | solution.py:99
  567.9 208.6 %all-gather.24.cloned.1.call-start = ((), (), s32[]{:S(2)}) async-start(), calls=%async_computation.19 | async-start | bytes 2621440 | tf_op jit(solution)/shard_map/backward_attention/all_gather | solution.py:99
  649.2 269.6 %reduce-scatter.11.cloned.1.call-start = ((), (), s32[]{:S(2)}) async-start(), calls=%async_computation.24 | async-start | bytes 2359296 | tf_op jit(solution)/shard_map/weight_grads/reduce_scatter | solution.py:329
  662.8 257.9 %reduce-scatter.9.cloned.1.call-start = ((), (), s32[]{:S(2)}) async-start(), calls=%async_computation.23 | async-start | bytes 2359296 | tf_op jit(solution)/shard_map/weight_grads/reduce_scatter | solution.py:329
  771.0 8.9 collective-permute-start.6
  773.6 7.5 collective-permute-start.7
  787.9 120.2 %all-to-all-start.8 = ((bf16[1,4,256,1024]{3,2,0,1:T(8,128)(2,1)}), bf16[1,4,256,1024]{3,2,0,1:T(8,128)(2,1)}, u32[]{:S(2)}, u32[]{:S(2)}) async-start(bf16[1,4,256,1024]{3,2,0,1:T(8,128)(2,1)} %bitcast.685), calls=%async_computation.8 | async-start | bytes 4194304 | tf_op jit(solution)/shard_map/backward_attention/all_to_all | solution.py:105
  792.6 140.3 %reduce-scatter.7.cloned.1.call-start = ((), (), s32[]{:S(2)}) async-start(), calls=%async_computation.22 | async-start | bytes 589824 | tf_op jit(solution)/shard_map/weight_grads/reduce_scatter | solution.py:329
  882.4 14.8 %collective-permute-start.4 = (bf16[1,1024,256]{2,1,0:T(8,128)(2,1)}, bf16[1,1024,256]{2,1,0:T(8,128)(2,1)}, u32[]{:S(2)}, u32[]{:S(2)}) collective-permute-start(bf16[1,1024,256]{2,1,0:T(8,128)(2,1)} %copy.340), channel_id=1, source_target_pairs={{0,4},{4,0},{1,5},{5,1},{2,6},{6,2},{3,7},{7,3},{8,12},{12,8},{9,1... | collective-permute-start | bytes 1572872 | tf_op jit(solution)/shard_map/backward_attention/ppermute | solution.py:89
  886.0 12.4 %collective-permute-start.5 = (bf16[1,1024,256]{2,1,0:T(8,128)(2,1)}, bf16[1,1024,256]{2,1,0:T(8,128)(2,1)}, u32[]{:S(2)}, u32[]{:S(2)}) collective-permute-start(bf16[1,1024,256]{2,1,0:T(8,128)(2,1)} %copy.342), channel_id=1, source_target_pairs={{0,4},{4,0},{1,5},{5,1},{2,6},{6,2},{3,7},{7,3},{8,12},{12,8},{9,1... | collective-permute-start | bytes 1572872 | tf_op jit(solution)/shard_map/backward_attention/ppermute | solution.py:89
  908.1 71.3 %all-to-all-start.6 = ((bf16[1,4,256,1024]{3,2,0,1:T(8,128)(2,1)}), bf16[1,4,256,1024]{3,2,0,1:T(8,128)(2,1)}, u32[]{:S(2)}, u32[]{:S(2)}) async-start(bf16[1,4,256,1024]{3,2,0,1:T(8,128)(2,1)} %bitcast.93), calls=%async_computation.6 | async-start | bytes 4194304 | tf_op jit(solution)/shard_map/backward_attention/all_to_all | solution.py:105
  913.3 61.4 %reduce-scatter.5.cloned.1.call-start = ((), (), s32[]{:S(2)}) async-start(), calls=%async_computation.21 | async-start | bytes 1769472 | tf_op jit(solution)/shard_map/weight_grads/reduce_scatter | solution.py:329
  918.8 60.4 %copy-start.69 = (f32[1,1,1,1024]{3,1,2,0:T(1,128)S(1)}, f32[1,1,1,1024]{3,1,2,0:T(1,128)}, u32[]{:S(2)}) copy-start(f32[1,1,1,1024]{3,1,2,0:T(1,128)} %get-tuple-element.633) | copy-start | bytes 12292
  918.8 63.5 %copy-start.84 = (f32[256]{0:T(256)}, f32[256]{0:T(256)S(1)}, u32[]{:S(2)}) copy-start(f32[256]{0:T(256)S(1)} %add_rsqrt_fusion.2) | copy-start | bytes 3076
  918.8 63.5 %copy-start.85 = (f32[256]{0:T(256)}, f32[256]{0:T(256)S(1)}, u32[]{:S(2)}) copy-start(f32[256]{0:T(256)S(1)} %add_rsqrt_fusion.3) | copy-start | bytes 3076
  923.5 58.6 %copy-start.70 = (f32[1,1,1,1024]{3,1,2,0:T(1,128)S(1)}, f32[1,1,1,1024]{3,1,2,0:T(1,128)}, u32[]{:S(2)}) copy-start(f32[1,1,1,1024]{3,1,2,0:T(1,128)} %get-tuple-element.629) | copy-start | bytes 12292
  988.9 10.4 %all-to-all-start.9 = ((f32[4,1,3072]{2,1,0:T(1,128)}), f32[4,1,3072]{2,1,0:T(1,128)}, u32[]{:S(2)}, u32[]{:S(2)}) async-start(f32[4,1,3072]{2,1,0:T(1,128)} %reshape.1457), calls=%async_computation.13 | async-start | bytes 98304 | tf_op jit(solution)/shard_map/ada_grad/all_to_all | solution.py:318
  993.5 20.9 %copy-start.1 = (bf16[128,6,256]{2,0,1:T(8,128)(2,1)S(1)}, bf16[128,6,256]{2,0,1:T(8,128)(2,1)}, u32[]{:S(2)}) copy-start(bf16[128,6,256]{2,0,1:T(8,128)(2,1)} %param.23) | copy-start | bytes 1179652
  996.2 16.8 %copy-start.68 = (bf16[8,2,4,128]{3,0,2,1:T(8,128)(2,1)S(1)}, bf16[8,2,4,128]{3,0,2,1:T(8,128)(2,1)}, u32[]{:S(2)}) copy-start(bf16[8,2,4,128]{3,0,2,1:T(8,128)(2,1)} %copy-done.67) | copy-start | bytes 49156
  (85 other events, 505.3 us)
Sparse Core Ops, SparseCore 0:
  9.6 87.6 all-gather.27
  99.7 24.2 all-gather.13
  125.6 119.1 all-gather.29
  246.5 26.3 all-gather.19
  274.6 27.7 all-gather.17
  311.3 44.8 all-gather.21
  358.4 79.0 all-gather.15
  568.0 74.0 all-gather.25
  649.4 43.9 all-gather.23
  696.4 39.9 reduce-scatter.10
  739.7 41.1 reduce-scatter.8
  897.3 35.5 reduce-scatter.6
  936.2 38.3 reduce-scatter.4
where the time goes:
time: 1030 us; the launch traced here: 1020 us
  waiting for transfers between devices  430 us (42%)
  matrix products  264 us (26%)
  other arithmetic  141 us (14%)
  local copies, waits for them, and re-layouts  68 us (7%)
  blocking collectives  52.3 us (5%)
  starting transfers between devices  48.6 us (5%)
  between operations  15.9 us (2%)
    all_to_all x8, waiting for transfers between devices, scatter_tokens(): received = lax.all_to_all(parts, 'tensor', 1, 1, tiled=True)  237 us
    all_gather x4, waiting for transfers between devices, gather_tokens(): return lax.all_gather(values, 'tensor', axis=1, tiled=True)  86.3 us
    reduce_scatter x4, waiting for transfers between devices, on_device(): lax.psum_scatter(total.astype(jnp.bfloat16), ('dp', 'frame'), scatter_dim...  49.6 us
    convert_element_type x4, other arithmetic, attend_back(): grad_scores = (probs * (grad_probs - row_terms)).astype(jnp.bfloat16)  41.9 us
    all_to_all x8, starting transfers between devices, scatter_tokens(): received = lax.all_to_all(parts, 'tensor', 1, 1, tiled=True)  37.6 us
    all_gather x1, waiting for transfers between devices, on_device(): group_tokens = lax.all_gather(tokens[:, 0], 'tensor', axis=1, tiled=True)  36.2 us
    dot_general x4, matrix products, attend_back(): jnp.einsum('cqhe,ckhe->chqk', grad_block, value_heads, preferred_element_...  34.3 us
    dot_general x4, matrix products, attend_back(): jnp.einsum('chqk,ckhe->cqhe', grad_scores, key_heads, preferred_element_t...  30 us
  transfers between devices with their start and end apart: 31, of which 12 were waited for; matrix products, arithmetic and copies ran while one was open for 43% of the time, Pallas kernels for 0%

commit v1 on v0

--- a/solution.py
+++ b/solution.py
@@ -1,3 +1,4 @@
+import functools
 import math
 import jax
 import jax.numpy as jnp
@@ -7,6 +8,22 @@
 HEAD_DIM = 64
 epsilon = 1e-06
 highest = lax.Precision.HIGHEST
+
+
+def fill_shards(frame_in, lane_axis):
+    local_now, after = (lax.axis_size(lane_axis), lax.axis_index(lane_axis))
+    even, v_next = (frame_in, 1)
+    while v_next < local_now:
+        spare = range(local_now)
+        val = lax.ppermute(even, lane_axis, list(map(lambda q: (q, q ^ v_next), spare)))
+        clean = jnp.concatenate([even, val], axis=0)
+        aux = jnp.concatenate([val, even], axis=0)
+        even = jnp.where(after & v_next == 0, clean, aux)
+        v_next = 2 * v_next
+    return even
+
+
+attach_zone = functools.partial(fill_shards, lane_axis=("dp", "frame"))
 
 
 def normalize(values):
@@ -64,8 +81,7 @@
         modulation = lax.dynamic_index_in_dim(group_mod, group_index, axis=2, keepdims=False)
     with jax.named_scope("weights"):
         joint_weight, mixer_weight, upward_weight, downward_weight = (
-            lax.all_gather(w, ("dp", "frame"), axis=0, tiled=True)
-            for w in (qkv_weight, out_weight, up_weight, down_weight)
+            attach_zone(w) for w in (qkv_weight, out_weight, up_weight, down_weight)
         )
     residual = tokens[:, 0].astype(jnp.float32)
     upstream = out_grad[:, 0].astype(jnp.float32)

time: 1030 us -> 991 us (0.962)
  waiting for transfers between devices: 430 us -> 406 us
  local copies, waits for them, and re-layouts: 68 us -> 54.7 us
  blocking collectives: 52.3 us -> 39 us
  starting transfers between devices: 48.6 us -> 59.9 us
    all_gather x4, waiting for transfers between devices: 86.3 us -> 24.1 us  [gather_tokens(): return lax.all_gather(values, 'tensor', axis=1, tiled=True)]
    ppermute x0 -> x12, waiting for transfers between devices: none -> 43.3 us  [fill_shards(): lax.ppermute(even, lane_axis, list(map(lambda q: (q, q ^ v_next), spare)))]
    all_gather x3 -> x0, waiting for transfers between devices: 16.2 us -> none  [on_device(): lax.all_gather(w, ('dp', 'frame'), axis=0, tiled=True)]
    all_gather x1 -> x0, blocking collectives: 12.8 us -> none  [on_device(): lax.all_gather(w, ('dp', 'frame'), axis=0, tiled=True)]
    ppermute x0 -> x12, starting transfers between devices: none -> 11.7 us  [fill_shards(): lax.ppermute(even, lane_axis, list(map(lambda q: (q, q ^ v_next), spare)))]
    unnamed x204 -> x229, local copies, waits for them, and re-layouts: 28 us -> 25.1 us
  transfers between devices with their start and end apart: 31 -> 40, of which waited for: 12 -> 18; matrix products, arithmetic and copies ran while one was open for 43% -> 43% of each run, Pallas kernels for 0% -> 0%
where the time goes in v1:
time: 991 us; the launch traced here: 980 us
  waiting for transfers between devices  406 us (41%)
  matrix products  261 us (26%)
  other arithmetic  143 us (14%)
  starting transfers between devices  59.9 us (6%)
  local copies, waits for them, and re-layouts  54.7 us (6%)
  blocking collectives  39 us (4%)
  between operations  16.5 us (2%)
    all_to_all x8, waiting for transfers between devices, scatter_tokens(): received = lax.all_to_all(parts, 'tensor', 1, 1, tiled=True)  240 us
    reduce_scatter x4, waiting for transfers between devices, on_device(): lax.psum_scatter(total.astype(jnp.bfloat16), ('dp', 'frame'), scatter_dim...  50.9 us
    ppermute x12, waiting for transfers between devices, fill_shards(): lax.ppermute(even, lane_axis, list(map(lambda q: (q, q ^ v_next), spare)))  43.3 us
    convert_element_type x4, other arithmetic, attend_back(): grad_scores = (probs * (grad_probs - row_terms)).astype(jnp.bfloat16)  41.9 us
    all_gather x1, waiting for transfers between devices, on_device(): group_tokens = lax.all_gather(tokens[:, 0], 'tensor', axis=1, tiled=True)  41.1 us
    all_to_all x8, starting transfers between devices, scatter_tokens(): received = lax.all_to_all(parts, 'tensor', 1, 1, tiled=True)  37.3 us
    dot_general x4, matrix products, attend_back(): jnp.einsum('cqhe,ckhe->chqk', grad_block, value_heads, preferred_element_...  34.3 us
    dot_general x4, matrix products, attend_back(): jnp.einsum('chqk,ckhe->cqhe', grad_scores, key_heads, preferred_element_t...  30.1 us
  transfers between devices with their start and end apart: 40, of which 18 were waited for; matrix products, arithmetic and copies ran while one was open for 43% of the time, Pallas kernels for 0%

profile of v1, /device:TPU:0, one launch (start us, length us, event | category | flops | bytes accessed | tf_op | source)
XLA Modules:
  0.0 979.9 jit_solution(3880863354238048014)
XLA Ops:
  8.5 10.1 %all-gather.3 = s32[8,2,4]{2,1,0:T(2,128)S(1)} all-gather(s32[1,2,4]{2,1,0:T(2,128)} %bitcast.719), channel_id=1, replica_groups=mesh['dp'=4,'frame'=2,'tensor'=4] {'dp','frame'}, dimensions={0}, use_global_device_ids=true | all-gather | bytes 288 | tf_op jit(solution)/shard_map/modulation/all_gather | solution.py:67
  35.0 19.4 %all_gather.28 = f32[2,4,6,1024]{3,2,1,0:T(8,128)S(1)} all-gather(f32[2,4,6,256]{3,2,1,0:T(8,128)S(1)} %copy.329), channel_id=1, replica_groups=mesh['dp'=4,'frame'=2,'tensor'=4] {'tensor'}, dimensions={3}, use_global_device_ids=true | all-gather | bytes 245760 | tf_op jit(solution)/shard_map/modulation/all_gather | solution.py:78
  56.1 41.1 %all-gather.19.cloned.1.call-done = bf16[2,1,1024,1024]{3,2,1,0:T(8,128)(2,1)} async-done(((bf16[2,1,256,1024]{3,2,1,0:T(8,128)(2,1)}), bf16[2,1,1024,1024]{3,2,1,0:T(8,128)(2,1)}) %all-gather.19.cloned.1.call-update) | async-done | bytes 4194320 | tf_op jit(solution)/shard_map/group_inputs/all_gather | solution.py:89
  124.6 20.7 %while.55 = (s32[]{:T(128)}, bf16[2,1,512,4,64]{2,4,3,1,0:T(8,128)(2,1)S(1)}, f32[2,1,4,512]{3,2,1,0:T(4,128)S(1)}, bf16[2,1,512,4,64]{2,4,3,1,0:T(8,128)(2,1)S(...) while((s32[]{:T(128)}, ...), condition=%wide.region_16.17_spmd, body=%wide.region_13.16_spmd.sunk | while | flops 1111619584 | bytes 53018712 | solution.py:168
  157.6 20.6 %while.54 = (s32[]{:T(128)}, bf16[2,1,512,4,64]{2,4,3,1,0:T(8,128)(2,1)S(1)}, f32[2,1,4,512]{3,2,1,0:T(4,128)S(1)}, bf16[2,1,512,4,64]{2,4,3,1,0:T(8,128)(2,1)S(...) while((s32[]{:T(128)}, ...), condition=%wide.region_6.7_spmd, body=%wide.region_3.6_spmd.sunk | while | flops 1111619584 | bytes 53018712 | solution.py:168
  183.1 39.6 %all-to-all-done.3 = bf16[1,4,256,1024]{3,2,0,1:T(8,128)(2,1)} async-done(((bf16[1,4,256,1024]{3,2,0,1:T(8,128)(2,1)}), bf16[1,4,256,1024]{3,2,0,1:T(8,128)(2,1)}, u32[]{:S(2)}, u32[]{:S(2)}) %all-to-all-start.3) | async-done | bytes 2097184 | tf_op jit(solution)/shard_map/forward/all_to_all | solution.py:121
  232.0 43.7 %all-to-all-done.1 = bf16[1,4,256,1024]{3,2,0,1:T(8,128)(2,1)} async-done(((bf16[1,4,256,1024]{3,2,0,1:T(8,128)(2,1)}), bf16[1,4,256,1024]{3,2,0,1:T(8,128)(2,1)}, u32[]{:S(2)}, u32[]{:S(2)}) %all-to-all-start.1) | async-done | bytes 2097184 | tf_op jit(solution)/shard_map/forward/all_to_all | solution.py:121
  286.1 11.9 %collective-permute-done.9 = bf16[256,1024]{1,0:T(8,128)(2,1)S(1)} collective-permute-done((bf16[256,1024]{1,0:T(8,128)(2,1)S(1)}, bf16[256,1024]{1,0:T(8,128)(2,1)S(1)}, u32[]{:S(2)}, u32[]{:S(2)}) %collective-permute-start.9) | collective-permute-done | bytes 524320 | tf_op jit(solution)/shard_map/weights/ppermute | solution.py:18
  301.0 7.4 collective-permute-done.12
  310.5 5.6 fusion.107
  317.4 8.5 collective-permute-done.10
  326.2 5.3 fusion.140
  331.5 14.4 %collective-permute-done.13 = bf16[512,1024]{1,0:T(8,128)(2,1)} collective-permute-done((bf16[512,1024]{1,0:T(8,128)(2,1)S(1)}, bf16[512,1024]{1,0:T(8,128)(2,1)}, u32[]{:S(2)}, u32[]{:S(2)}) %collective-permute-start.13) | collective-permute-done | bytes 1048608 | tf_op jit(solution)/shard_map/weights/ppermute | solution.py:18
  345.9 6.0 fusion.125
  352.0 6.6 convolution_convert_fusion
  363.5 23.8 %all-gather.11.cloned.1.call-done = bf16[1,1024,1024]{2,1,0:T(8,128)(2,1)} async-done(((bf16[1,256,1024]{2,1,0:T(8,128)(2,1)}), bf16[1,1024,1024]{2,1,0:T(8,128)(2,1)}) %all-gather.11.cloned.1.call-update) | async-done | bytes 2097168 | tf_op jit(solution)/shard_map/forward/all_gather | solution.py:115
  387.3 5.3 fusion.144
  392.6 6.8 fusion.118
  400.7 6.0 convolution_convert_fusion.1
  406.7 10.6 %all-to-all-done.7 = bf16[1,4,256,1024]{3,2,0,1:T(8,128)(2,1)} async-done(((bf16[1,4,256,1024]{3,2,0,1:T(8,128)(2,1)}), bf16[1,4,256,1024]{3,2,0,1:T(8,128)(2,1)}, u32[]{:S(2)}, u32[]{:S(2)}) %all-to-all-start.7) | async-done | bytes 2097184 | tf_op jit(solution)/shard_map/backward_ffn/all_to_all | solution.py:121
  421.8 7.7 convolution_convert_fusion.2
  429.5 40.7 %all-to-all-done.5 = bf16[1,4,256,1024]{3,2,0,1:T(8,128)(2,1)} async-done(((bf16[1,4,256,1024]{3,2,0,1:T(8,128)(2,1)}), bf16[1,4,256,1024]{3,2,0,1:T(8,128)(2,1)}, u32[]{:S(2)}, u32[]{:S(2)}) %all-to-all-start.5) | async-done | bytes 2097184 | tf_op jit(solution)/shard_map/backward_ffn/all_to_all | solution.py:121
  476.3 8.3 convolution_convert_fusion.4
  484.6 38.0 %all-to-all-done.4 = bf16[1,4,256,1024]{3,2,0,1:T(8,128)(2,1)} async-done(((bf16[1,4,256,1024]{3,2,0,1:T(8,128)(2,1)}), bf16[1,4,256,1024]{3,2,0,1:T(8,128)(2,1)}, u32[]{:S(2)}, u32[]{:S(2)}) %all-to-all-start.4) | async-done | bytes 2097184 | tf_op jit(solution)/shard_map/forward/all_to_all | solution.py:121
  541.2 67.0 %all-to-all-done.2 = bf16[1,4,256,1024]{3,2,0,1:T(8,128)(2,1)} async-done(((bf16[1,4,256,1024]{3,2,0,1:T(8,128)(2,1)}), bf16[1,4,256,1024]{3,2,0,1:T(8,128)(2,1)}, u32[]{:S(2)}, u32[]{:S(2)}) %all-to-all-start.2) | async-done | bytes 2097184 | tf_op jit(solution)/shard_map/forward/all_to_all | solution.py:121
  644.7 87.0 %while.57 = (s32[]{:T(128)}, f32[1,2048,4,64]{1,3,2,0:T(8,128)}, f32[1,2048,4,64]{1,3,2,0:T(8,128)}, bf16[2,1,512,4,64]{2,4,3,1,0:T(8,128)(2,1)}, bf16[2,1,512,4...) while((s32[]{:T(128)}, f32[1,2048,4,64]{1,3,2,0:T(8,128)}, ...), condition=%wide.region_39.40_spmd.clone, body=%wide.region_37.39_spmd.clone.sunk | while | flops 2737436672 | bytes 273212096 | solution.py:279
  647.1 8.6 multiply_reduce_fusion.23
  658.0 10.5 %multiply_convert_fusion.14 = bf16[4,512,2048]{2,1,0:T(8,128)(2,1)} fusion(f32[4,512,2048]{2,1,0:T(8,128)} %get-tuple-element.844, f32[4,512,2048]{2,1,0:T(8,128)S(1)} %fusion.288, f32[4,512]{1,0:T(4,128)S(1)} %get-tuple-element.845, f32[4,512]{1,0:T(4,128)S(1)} %dynamic-slice_bitcast_fusion.7), kind=kLoop, calls=%fused_computation.66.clone.1 | loop fusion | flops 20971520 | bytes 41959424 | tf_op jit(solution)/shard_map/backward_attention/while/body/eval_jaxpr/convert_element_type | solution.py:256
  668.4 6.9 fusion.289
  675.3 7.5 fusion.291
  689.6 8.6 multiply_reduce_fusion.23
  700.5 10.5 %multiply_convert_fusion.14 = bf16[4,512,2048]{2,1,0:T(8,128)(2,1)} fusion(f32[4,512,2048]{2,1,0:T(8,128)} %get-tuple-element.844, f32[4,512,2048]{2,1,0:T(8,128)S(1)} %fusion.288, f32[4,512]{1,0:T(4,128)S(1)} %get-tuple-element.845, f32[4,512]{1,0:T(4,128)S(1)} %dynamic-slice_bitcast_fusion.7), kind=kLoop, calls=%fused_computation.66.clone.1 | loop fusion | flops 20971520 | bytes 41959424 | tf_op jit(solution)/shard_map/backward_attention/while/body/eval_jaxpr/convert_element_type | solution.py:256
  711.0 7.5 fusion.289
  718.5 7.6 fusion.291
  726.0 5.6 fusion.290
  755.9 86.0 %while.56 = (s32[]{:T(128)}, f32[1,2048,4,64]{1,3,2,0:T(8,128)}, f32[1,2048,4,64]{1,3,2,0:T(8,128)}, bf16[2,1,512,4,64]{2,4,3,1,0:T(8,128)(2,1)}, bf16[2,1,512,4...) while((s32[]{:T(128)}, f32[1,2048,4,64]{1,3,2,0:T(8,128)}, ...), condition=%wide.region_28.29_spmd.clone, body=%wide.region_26.28_spmd.clone.sunk | while | flops 2737436672 | bytes 273212096 | solution.py:279
  758.4 8.6 multiply_reduce_fusion.22
  769.3 10.5 %multiply_convert_fusion.13 = bf16[4,512,2048]{2,1,0:T(8,128)(2,1)} fusion(f32[4,512,2048]{2,1,0:T(8,128)} %get-tuple-element.833, f32[4,512,2048]{2,1,0:T(8,128)S(1)} %fusion.276, f32[4,512]{1,0:T(4,128)S(1)} %get-tuple-element.834, f32[4,512]{1,0:T(4,128)S(1)} %dynamic-slice_bitcast_fusion.6), kind=kLoop, calls=%fused_computation.32.clone.1 | loop fusion | flops 20971520 | bytes 41959424 | tf_op jit(solution)/shard_map/backward_attention/while/body/eval_jaxpr/convert_element_type | solution.py:256
  779.7 6.5 fusion.277
  786.2 7.5 fusion.279
  800.5 8.6 multiply_reduce_fusion.22
  811.4 10.5 %multiply_convert_fusion.13 = bf16[4,512,2048]{2,1,0:T(8,128)(2,1)} fusion(f32[4,512,2048]{2,1,0:T(8,128)} %get-tuple-element.833, f32[4,512,2048]{2,1,0:T(8,128)S(1)} %fusion.276, f32[4,512]{1,0:T(4,128)S(1)} %get-tuple-element.834, f32[4,512]{1,0:T(4,128)S(1)} %dynamic-slice_bitcast_fusion.6), kind=kLoop, calls=%fused_computation.32.clone.1 | loop fusion | flops 20971520 | bytes 41959424 | tf_op jit(solution)/shard_map/backward_attention/while/body/eval_jaxpr/convert_element_type | solution.py:256
  821.8 7.0 fusion.277
  828.9 7.5 fusion.279
  836.4 5.6 fusion.278
  880.5 10.9 %reduce-scatter.7.cloned.1.call-done = bf16[128,256]{1,0:T(8,128)(2,1)} async-done(((bf16[1024,256]{1,0:T(8,128)(2,1)}), bf16[128,256]{1,0:T(8,128)(2,1)}) %reduce-scatter.7.cloned.1.call-update) | async-done | bytes 65552 | tf_op jit(solution)/shard_map/weight_grads/reduce_scatter | solution.py:345
  892.8 40.0 %reduce-scatter.5.cloned.1.call-done = bf16[128,3,256]{2,0,1:T(8,128)(2,1)} async-done(((bf16[1024,3,256]{2,0,1:T(8,128)(2,1)}), bf16[128,3,256]{2,0,1:T(8,128)(2,1)}) %reduce-scatter.5.cloned.1.call-update) | async-done | bytes 196624 | tf_op jit(solution)/shard_map/weight_grads/reduce_scatter | solution.py:345
  961.6 9.5 all-gather.2
  (499 shorter events, 323.7 us)
Async XLA Ops:
  7.2 90.0 %all-gather.19.cloned.1.call-start = ((), (), s32[]{:S(2)}) async-start(), calls=%async_computation.22 | async-start | bytes 5242880 | tf_op jit(solution)/shard_map/group_inputs/all_gather | solution.py:89
  7.9 11.4 %collective-permute-start.5 = (bf16[128,256]{1,0:T(8,128)(2,1)}, bf16[128,256]{1,0:T(8,128)(2,1)S(1)}, u32[]{:S(2)}, u32[]{:S(2)}) collective-permute-start(bf16[128,256]{1,0:T(8,128)(2,1)} %param.20), channel_id=1, source_target_pairs={{0,4},{4,0},{8,12},{12,8},{16,20},{20,16},{24,28},{28,24},{1,5},{5... | collective-permute-start | bytes 196616 | tf_op jit(solution)/shard_map/weights/ppermute | solution.py:18
  20.2 6.6 collective-permute-start.6
  22.6 12.3 %all-to-all-start = ((f32[8,2,4,6,256]{4,2,3,1,0:T(4,128)}), f32[8,2,4,6,256]{4,2,3,1,0:T(4,128)S(1)}, u32[]{:S(2)}, u32[]{:S(2)}) async-start(f32[8,2,4,6,256]{4,2,3,1,0:T(4,128)} %fusion.183), calls=%async_computation | async-start | bytes 786432 | tf_op jit(solution)/shard_map/modulation/all_to_all | solution.py:77
  26.1 284.4 %all-gather.21.cloned.1.call-start = ((), (), s32[]{:S(2)}) async-start(), calls=%async_computation.23 | async-start | bytes 5242880 | tf_op jit(solution)/shard_map/group_inputs/all_gather | solution.py:90
  26.1 3.5 collective-permute-start
  27.7 118.4 %collective-permute-start.7 = (bf16[512,256]{1,0:T(8,128)(2,1)}, bf16[512,256]{1,0:T(8,128)(2,1)}, u32[]{:S(2)}, u32[]{:S(2)}) collective-permute-start(bf16[512,256]{1,0:T(8,128)(2,1)} %maximum_select_fusion.10), channel_id=1, source_target_pairs={{0,16},{4,20},{8,24},{12,28},{16,0},{20,4},{24,8},{28,12},{1,17},{... | collective-permute-start | bytes 786440 | tf_op jit(solution)/shard_map/weights/ppermute | solution.py:18
  29.8 26.0 %collective-permute-start.1 = (bf16[256,3,256]{2,0,1:T(8,128)(2,1)S(1)}, bf16[256,3,256]{2,0,1:T(8,128)(2,1)S(1)}, u32[]{:S(2)}, u32[]{:S(2)}) collective-permute-start(bf16[256,3,256]{2,0,1:T(8,128)(2,1)S(1)} %maximum_select_fusion.9), channel_id=1, source_target_pairs={{0,8},{4,12},{8,0},{12,4},{16,24},{20,28},{24,16},{28,20},{1,9},{5... | collective-permute-start | bytes 1179656 | tf_op jit(solution)/shard_map/weights/ppermute | solution.py:18
  56.0 51.2 %collective-permute-start.2 = (bf16[512,3,256]{2,0,1:T(8,128)(2,1)S(1)}, bf16[512,3,256]{2,0,1:T(8,128)(2,1)S(1)}, u32[]{:S(2)}, u32[]{:S(2)}) collective-permute-start(bf16[512,3,256]{2,0,1:T(8,128)(2,1)S(1)} %maximum_select_fusion.5), channel_id=1, source_target_pairs={{0,16},{4,20},{8,24},{12,28},{16,0},{20,4},{24,8},{28,12},{1,17},{... | collective-permute-start | bytes 2359304 | tf_op jit(solution)/shard_map/weights/ppermute | solution.py:18
  112.9 8.5 collective-permute-start.15
  112.9 10.6 %collective-permute-start.14 = (bf16[1,1024,256]{1,2,0:T(8,128)(2,1)}, bf16[1,1024,256]{1,2,0:T(8,128)(2,1)}, u32[]{:S(2)}, u32[]{:S(2)}) collective-permute-start(bf16[1,1024,256]{1,2,0:T(8,128)(2,1)} %get-tuple-element.606), channel_id=1, source_target_pairs={{0,4},{4,0},{1,5},{5,1},{2,6},{6,2},{3,7},{7,3},{8,12},{12,8},{9,1... | collective-permute-start | bytes 1572872 | tf_op jit(solution)/shard_map/forward/ppermute | solution.py:95
  119.6 35.5 %collective-permute-start.4 = (bf16[1,1024,256]{1,2,0:T(8,128)(2,1)}, bf16[1,1024,256]{1,2,0:T(8,128)(2,1)}, u32[]{:S(2)}, u32[]{:S(2)}) collective-permute-start(bf16[1,1024,256]{1,2,0:T(8,128)(2,1)} %get-tuple-element.602), channel_id=1, source_target_pairs={{0,4},{4,0},{1,5},{5,1},{2,6},{6,2},{3,7},{7,3},{8,12},{12,8},{9,1... | collective-permute-start | bytes 1572872 | tf_op jit(solution)/shard_map/forward/ppermute | solution.py:95
  119.6 36.8 %collective-permute-start.3 = (bf16[1,1024,256]{1,2,0:T(8,128)(2,1)}, bf16[1,1024,256]{1,2,0:T(8,128)(2,1)}, u32[]{:S(2)}, u32[]{:S(2)}) collective-permute-start(bf16[1,1024,256]{1,2,0:T(8,128)(2,1)} %get-tuple-element.601), channel_id=1, source_target_pairs={{0,4},{4,0},{1,5},{5,1},{2,6},{6,2},{3,7},{7,3},{8,12},{12,8},{9,1... | collective-permute-start | bytes 1572872 | tf_op jit(solution)/shard_map/forward/ppermute | solution.py:95
  150.4 72.2 %all-to-all-start.3 = ((bf16[1,4,256,1024]{3,2,0,1:T(8,128)(2,1)}), bf16[1,4,256,1024]{3,2,0,1:T(8,128)(2,1)}, u32[]{:S(2)}, u32[]{:S(2)}) async-start(bf16[1,4,256,1024]{3,2,0,1:T(8,128)(2,1)} %bitcast.664), calls=%async_computation.3 | async-start | bytes 4194304 | tf_op jit(solution)/shard_map/forward/all_to_all | solution.py:121
  179.7 47.7 %copy-start.35 = (bf16[2,1,256,1024]{3,2,1,0:T(8,128)(2,1)S(1)}, bf16[2,1,256,1024]{3,2,1,0:T(8,128)(2,1)}, u32[]{:S(2)}) copy-start(bf16[2,1,256,1024]{3,2,1,0:T(8,128)(2,1)} %param.16) | copy-start | bytes 3145732
  222.7 53.0 %all-to-all-start.1 = ((bf16[1,4,256,1024]{3,2,0,1:T(8,128)(2,1)}), bf16[1,4,256,1024]{3,2,0,1:T(8,128)(2,1)}, u32[]{:S(2)}, u32[]{:S(2)}) async-start(bf16[1,4,256,1024]{3,2,0,1:T(8,128)(2,1)} %bitcast.666), calls=%async_computation.1 | async-start | bytes 4194304 | tf_op jit(solution)/shard_map/forward/all_to_all | solution.py:121
  227.1 99.1 %all-gather.13.cloned.1.call-start = ((), (), s32[]{:S(2)}) async-start(), calls=%async_computation.15 | async-start | bytes 2621440 | tf_op jit(solution)/shard_map/forward/all_gather | solution.py:115
  227.6 50.2 %copy-start.16 = (f32[2,1,256,1024]{3,2,1,0:T(8,128)}, f32[2,1,256,1024]{3,2,1,0:T(8,128)S(1)}, u32[]{:S(2)}) copy-start(f32[2,1,256,1024]{3,2,1,0:T(8,128)S(1)} %convert_element_type.357) | copy-start | bytes 6291460
  228.1 49.8 %copy-start.83 = (f32[256]{0:T(256)}, f32[256]{0:T(256)S(1)}, u32[]{:S(2)}) copy-start(f32[256]{0:T(256)S(1)} %get-tuple-element.640) | copy-start | bytes 3076
  228.1 49.8 %copy-start.85 = (f32[256]{0:T(256)}, f32[256]{0:T(256)S(1)}, u32[]{:S(2)}) copy-start(f32[256]{0:T(256)S(1)} %get-tuple-element.641) | copy-start | bytes 3076
  281.3 106.0 %all-gather.11.cloned.1.call-start = ((), (), s32[]{:S(2)}) async-start(), calls=%async_computation.14 | async-start | bytes 2621440 | tf_op jit(solution)/shard_map/forward/all_gather | solution.py:115
  281.4 1.6 collective-permute-start.8
  281.5 3.2 collective-permute-start.11
  283.1 14.9 %collective-permute-start.9 = (bf16[256,1024]{1,0:T(8,128)(2,1)S(1)}, bf16[256,1024]{1,0:T(8,128)(2,1)S(1)}, u32[]{:S(2)}, u32[]{:S(2)}) collective-permute-start(bf16[256,1024]{1,0:T(8,128)(2,1)S(1)} %maximum_select_fusion.7), channel_id=1, source_target_pairs={{0,8},{4,12},{8,0},{12,4},{16,24},{20,28},{24,16},{28,20},{1,9},{5... | collective-permute-start | bytes 1572872 | tf_op jit(solution)/shard_map/weights/ppermute | solution.py:18
  284.8 23.6 %collective-permute-start.12 = (bf16[256,1024]{1,0:T(8,128)(2,1)S(1)}, bf16[256,1024]{1,0:T(8,128)(2,1)S(1)}, u32[]{:S(2)}, u32[]{:S(2)}) collective-permute-start(bf16[256,1024]{1,0:T(8,128)(2,1)S(1)} %maximum_select_fusion.8), channel_id=1, source_target_pairs={{0,8},{4,12},{8,0},{12,4},{16,24},{20,28},{24,16},{28,20},{1,9},{5... | collective-permute-start | bytes 1572872 | tf_op jit(solution)/shard_map/weights/ppermute | solution.py:18
  299.5 26.3 %collective-permute-start.10 = (bf16[512,1024]{1,0:T(8,128)(2,1)}, bf16[512,1024]{1,0:T(8,128)(2,1)}, u32[]{:S(2)}, u32[]{:S(2)}) collective-permute-start(bf16[512,1024]{1,0:T(8,128)(2,1)} %maximum_select_fusion.3), channel_id=1, source_target_pairs={{0,16},{4,20},{8,24},{12,28},{16,0},{20,4},{24,8},{28,12},{1,17},{... | collective-permute-start | bytes 3145736 | tf_op jit(solution)/shard_map/weights/ppermute | solution.py:18
  308.9 112.9 %copy-start.52 = (bf16[512,1024]{1,0:T(8,128)(2,1)}, bf16[512,1024]{1,0:T(8,128)(2,1)S(1)}, u32[]{:S(2)}) copy-start(bf16[512,1024]{1,0:T(8,128)(2,1)S(1)} %maximum_select_fusion.4) | copy-start | bytes 3145732
  308.9 37.0 %collective-permute-start.13 = (bf16[512,1024]{1,0:T(8,128)(2,1)S(1)}, bf16[512,1024]{1,0:T(8,128)(2,1)}, u32[]{:S(2)}, u32[]{:S(2)}) collective-permute-start(bf16[512,1024]{1,0:T(8,128)(2,1)S(1)} %maximum_select_fusion.4), channel_id=1, source_target_pairs={{0,16},{4,20},{8,24},{12,28},{16,0},{20,4},{24,8},{28,12},{1,17},{... | collective-permute-start | bytes 3145736 | tf_op jit(solution)/shard_map/weights/ppermute | solution.py:18
  358.6 58.8 %all-to-all-start.7 = ((bf16[1,4,256,1024]{3,2,0,1:T(8,128)(2,1)}), bf16[1,4,256,1024]{3,2,0,1:T(8,128)(2,1)}, u32[]{:S(2)}, u32[]{:S(2)}) async-start(bf16[1,4,256,1024]{3,2,0,1:T(8,128)(2,1)} %bitcast.667), calls=%async_computation.7 | async-start | bytes 4194304 | tf_op jit(solution)/shard_map/backward_ffn/all_to_all | solution.py:121
  417.4 52.9 %all-to-all-start.5 = ((bf16[1,4,256,1024]{3,2,0,1:T(8,128)(2,1)}), bf16[1,4,256,1024]{3,2,0,1:T(8,128)(2,1)}, u32[]{:S(2)}, u32[]{:S(2)}) async-start(bf16[1,4,256,1024]{3,2,0,1:T(8,128)(2,1)} %bitcast.669), calls=%async_computation.5 | async-start | bytes 4194304 | tf_op jit(solution)/shard_map/backward_ffn/all_to_all | solution.py:121
  470.3 52.3 %all-to-all-start.4 = ((bf16[1,4,256,1024]{3,2,0,1:T(8,128)(2,1)}), bf16[1,4,256,1024]{3,2,0,1:T(8,128)(2,1)}, u32[]{:S(2)}, u32[]{:S(2)}) async-start(bf16[1,4,256,1024]{3,2,0,1:T(8,128)(2,1)} %bitcast.668), calls=%async_computation.4 | async-start | bytes 4194304 | tf_op jit(solution)/shard_map/forward/all_to_all | solution.py:121
  522.5 85.7 %all-to-all-start.2 = ((bf16[1,4,256,1024]{3,2,0,1:T(8,128)(2,1)}), bf16[1,4,256,1024]{3,2,0,1:T(8,128)(2,1)}, u32[]{:S(2)}, u32[]{:S(2)}) async-start(bf16[1,4,256,1024]{3,2,0,1:T(8,128)(2,1)} %bitcast.665), calls=%async_computation.2 | async-start | bytes 4194304 | tf_op jit(solution)/shard_map/forward/all_to_all | solution.py:121
  527.0 110.8 %all-gather.17.cloned.1.call-start = ((), (), s32[]{:S(2)}) async-start(), calls=%async_computation.17 | async-start | bytes 2621440 | tf_op jit(solution)/shard_map/backward_attention/all_gather | solution.py:115
  534.7 203.8 %all-gather.15.cloned.1.call-start = ((), (), s32[]{:S(2)}) async-start(), calls=%async_computation.16 | async-start | bytes 2621440 | tf_op jit(solution)/shard_map/backward_attention/all_gather | solution.py:115
  615.7 260.0 %reduce-scatter.11.cloned.1.call-start = ((), (), s32[]{:S(2)}) async-start(), calls=%async_computation.21 | async-start | bytes 2359296 | tf_op jit(solution)/shard_map/weight_grads/reduce_scatter | solution.py:345
  629.5 248.1 %reduce-scatter.9.cloned.1.call-start = ((), (), s32[]{:S(2)}) async-start(), calls=%async_computation.20 | async-start | bytes 2359296 | tf_op jit(solution)/shard_map/weight_grads/reduce_scatter | solution.py:345
  734.7 7.6 collective-permute-start.18
  736.1 7.4 collective-permute-start.19
  750.3 114.9 %all-to-all-start.8 = ((bf16[1,4,256,1024]{3,2,0,1:T(8,128)(2,1)}), bf16[1,4,256,1024]{3,2,0,1:T(8,128)(2,1)}, u32[]{:S(2)}, u32[]{:S(2)}) async-start(bf16[1,4,256,1024]{3,2,0,1:T(8,128)(2,1)} %bitcast.663), calls=%async_computation.8 | async-start | bytes 4194304 | tf_op jit(solution)/shard_map/backward_attention/all_to_all | solution.py:121
  755.0 136.3 %reduce-scatter.7.cloned.1.call-start = ((), (), s32[]{:S(2)}) async-start(), calls=%async_computation.19 | async-start | bytes 589824 | tf_op jit(solution)/shard_map/weight_grads/reduce_scatter | solution.py:345
  845.0 10.7 %collective-permute-start.16 = (bf16[1,1024,256]{2,1,0:T(8,128)(2,1)}, bf16[1,1024,256]{2,1,0:T(8,128)(2,1)}, u32[]{:S(2)}, u32[]{:S(2)}) collective-permute-start(bf16[1,1024,256]{2,1,0:T(8,128)(2,1)} %copy.332), channel_id=1, source_target_pairs={{0,4},{4,0},{1,5},{5,1},{2,6},{6,2},{3,7},{7,3},{8,12},{12,8},{9,1... | collective-permute-start | bytes 1572872 | tf_op jit(solution)/shard_map/backward_attention/ppermute | solution.py:105
  847.2 9.8 collective-permute-start.17
  865.2 72.2 %all-to-all-start.6 = ((bf16[1,4,256,1024]{3,2,0,1:T(8,128)(2,1)}), bf16[1,4,256,1024]{3,2,0,1:T(8,128)(2,1)}, u32[]{:S(2)}, u32[]{:S(2)}) async-start(bf16[1,4,256,1024]{3,2,0,1:T(8,128)(2,1)} %bitcast.93), calls=%async_computation.6 | async-start | bytes 4194304 | tf_op jit(solution)/shard_map/backward_attention/all_to_all | solution.py:121
  870.5 62.3 %reduce-scatter.5.cloned.1.call-start = ((), (), s32[]{:S(2)}) async-start(), calls=%async_computation.18 | async-start | bytes 1769472 | tf_op jit(solution)/shard_map/weight_grads/reduce_scatter | solution.py:345
  875.7 64.8 %copy-start.95 = (f32[256]{0:T(256)}, f32[256]{0:T(256)S(1)}, u32[]{:S(2)}) copy-start(f32[256]{0:T(256)S(1)} %add_rsqrt_fusion.2) | copy-start | bytes 3076
  875.7 64.8 %copy-start.96 = (f32[256]{0:T(256)}, f32[256]{0:T(256)S(1)}, u32[]{:S(2)}) copy-start(f32[256]{0:T(256)S(1)} %add_rsqrt_fusion.3) | copy-start | bytes 3076
  879.4 57.8 %copy-start.81 = (f32[1,1,1,1024]{3,1,2,0:T(1,128)S(1)}, f32[1,1,1,1024]{3,1,2,0:T(1,128)}, u32[]{:S(2)}) copy-start(f32[1,1,1,1024]{3,1,2,0:T(1,128)} %get-tuple-element.633) | copy-start | bytes 12292
  947.1 10.4 %all-to-all-start.9 = ((f32[4,1,3072]{2,1,0:T(1,128)}), f32[4,1,3072]{2,1,0:T(1,128)}, u32[]{:S(2)}, u32[]{:S(2)}) async-start(f32[4,1,3072]{2,1,0:T(1,128)} %reshape.1457), calls=%async_computation.13 | async-start | bytes 98304 | tf_op jit(solution)/shard_map/ada_grad/all_to_all | solution.py:334
  (107 other events, 855.2 us)
Sparse Core Ops, SparseCore 0:
  9.6 87.5 all-gather.18
  98.7 100.7 all-gather.20
  281.4 44.6 all-gather.12
  328.2 59.0 all-gather.10
  534.8 73.8 all-gather.16
  615.9 43.7 all-gather.14
  663.0 39.9 reduce-scatter.10
  706.2 41.1 reduce-scatter.8
  855.7 35.5 reduce-scatter.6
  894.5 38.3 reduce-scatter.4
